TPU v7x, 32 devices: a whole 2x2x4 slice. The times are simulated.
32 devices in a mesh: table: 16 (over z, y, x), dp: 2 (over core).
Axes of the slice: x: 2, y: 2, z: 4, core: 2. Of those that a mesh axis runs over, the one named last changes fastest.
Arguments:
- tables: bfloat16 [4, 65536, 128], P(None, 'table'), may hold values from -6 to 6
- owner_ids: int32 [32, 4, 256, 1], P(('table', 'dp')), may hold values from 0 to 15; in each aligned block of 256 rows (0 to 255, 256 to 511, ..., all dimensions but the last counted through in order) at most 32 rows name the same one
- row_ids: int32 [32, 4, 256], P(('table', 'dp')), may hold values from 0 to 4095
- session_of: int32 [32, 256], P(('table', 'dp')), may hold values from 0 to 1, never falling along the last dimension, each value on 1 to 200 neighbouring positions
- relevance: float32 [32, 256], P(('table', 'dp')), may hold values from 0.1 to 10
- logit_bias: float32 [32, 256], P(('table', 'dp')), may hold values from -400 to 400
- w_hidden: float32 [512, 512], replicated, may hold values from -0.25 to 0.25
- bias_hidden: float32 [512], replicated, may hold values from -3 to 3
- w_score: float32 [512], replicated, may hold values from -0.9 to 0.9
Outputs:
- emb_step: float32 [4, 65536, 128], P(None, ('table', 'dp'))
- step_hidden: float32 [512, 512], replicated
- step_bias: float32 [512], replicated
- step_score: float32 [512], replicated
- loss: float32 [], replicated
Inputs may be any that keep to these rules, and one draw needn't show every extreme that they name: `owner_ids`: among one device's impressions, for one table, at most 32 name the same owner. `session_of`: session numbers never fall along a device's impressions; each of a device's 2 sessions has 1 to 200 impressions.
All inputs are finite; a program needn't handle non-finite values.
Results may differ from a plain program's by a relative error of at most 0.001.
The roundings to bfloat16 on the way count: a program that leaves them out, or rounds other values in their place, can miss the bound.
Values may be sent and summed in bfloat16 or wider, within the bound.
A program may use at most 64 MiB of HBM per device.

v0:
```python
import jax
import jax.numpy as jnp
from jax import lax
from jax.sharding import PartitionSpec as P

SESS_DEV = 2


def silu_slope(pre_val):
    logistic = jax.nn.sigmoid(pre_val)
    return logistic * (1.0 + pre_val * (1.0 - logistic))


def session_terms(scores, session_ids, relevance, sessions):
    member = session_ids[None, :] == jnp.arange(sessions, dtype=jnp.int32)[:, None]
    highest = jnp.max(jnp.where(member, scores[None, :], -jnp.inf), axis=1)
    highest_each = jnp.sum(jnp.where(member, highest[:, None], 0.0), axis=0)
    shifted = scores - highest_each
    exponent = jnp.exp(shifted)
    totals = jnp.sum(jnp.where(member, exponent[None, :], 0.0), axis=1)
    weights = jnp.sum(jnp.where(member, relevance[None, :], 0.0), axis=1)
    total_each = jnp.sum(jnp.where(member, totals[:, None], 0.0), axis=0)
    weight_each = jnp.sum(jnp.where(member, weights[:, None], 0.0), axis=0)
    probability = exponent / total_each
    target = relevance / weight_each
    loss_sum = jnp.sum(jnp.log(totals)) - jnp.sum(target * shifted)
    return (loss_sum, probability - target)


def selector(indices, count):
    return (indices[:, None] == jnp.arange(count, dtype=jnp.int32)[None, :]).astype(jnp.bfloat16)


def pick_rows(indices, source):
    return jnp.dot(
        selector(indices, source.shape[0]), source, preferred_element_type=jnp.float32
    ).astype(jnp.bfloat16)


def place_rows(indices, values, count):
    return lax.dot_general(
        selector(indices, count),
        values,
        (((0,), (0,)), ((), ())),
        preferred_element_type=jnp.float32,
    )


def on_device(
    tables, owner_ids, row_ids, session_of, relevance, logit_bias, w_hidden, bias_hidden, w_score
):
    owners = lax.axis_size("table")
    devices = owners * lax.axis_size("dp")
    table_count, shard_rows, emb_width = tables.shape
    owner_now = owner_ids[0, :, :, 0]
    rows_now = row_ids[0]
    imp_count = owner_now.shape[1]
    capacity = 2 * imp_count // owners
    slot_total = owners * capacity
    one_hot = (owner_now[:, :, None] == jnp.arange(owners, dtype=jnp.int32)).astype(jnp.float32)
    places = jnp.arange(imp_count, dtype=jnp.int32)
    lower_tri = (places[:, None] >= places[None, :]).astype(jnp.float32)
    running = jnp.einsum("ij,tjo->tio", lower_tri, one_hot, precision=lax.Precision.HIGHEST)
    rank_in = (jnp.sum(running * one_hot, axis=2) - 1.0).astype(jnp.int32)
    slot_of = owner_now * capacity + rank_in
    slot_hot = (slot_of[:, :, None] == jnp.arange(slot_total, dtype=jnp.int32)).astype(jnp.int32)
    wanted = jnp.sum(slot_hot * rows_now[:, :, None], axis=1) + shard_rows * (
        1 - jnp.sum(slot_hot, axis=1)
    )
    requested = lax.all_to_all(
        wanted.reshape(table_count, owners, capacity),
        "table",
        split_axis=1,
        concat_axis=1,
        tiled=True,
    )
    served = lax.map(
        lambda pair: pick_rows(pair[0], pair[1]),
        (requested.reshape(table_count, slot_total), tables),
    )
    served = served.reshape(table_count, owners, capacity, emb_width)
    hidden_bf = w_hidden.astype(jnp.bfloat16)
    returned = lax.all_to_all(served, "table", split_axis=1, concat_axis=1, tiled=True).reshape(
        table_count, slot_total, emb_width
    )
    gathered = lax.map(lambda pair: pick_rows(pair[0], pair[1]), (slot_of, returned))
    inputs = jnp.transpose(gathered, (1, 0, 2)).reshape(imp_count, table_count * emb_width)
    pre_act = jnp.dot(inputs, hidden_bf, preferred_element_type=jnp.float32)
    pre_act = pre_act + bias_hidden
    hidden = jax.nn.silu(pre_act)
    scores = jnp.dot(hidden, w_score, precision=lax.Precision.HIGHEST) + logit_bias[0]
    loss_sum, score_grad = session_terms(scores, session_of[0], relevance[0], SESS_DEV)
    pre_grad = score_grad[:, None] * w_score[None, :] * silu_slope(pre_act)
    pre_grad_bf = pre_grad.astype(jnp.bfloat16)
    weight_grad = lax.dot_general(
        inputs, pre_grad_bf, (((0,), (0,)), ((), ())), preferred_element_type=jnp.float32
    )
    bias_grad = jnp.sum(pre_grad, axis=0)
    score_weight_grad = jnp.dot(score_grad, hidden, precision=lax.Precision.HIGHEST)
    input_grad = jnp.dot(pre_grad_bf, hidden_bf.T, preferred_element_type=jnp.float32).astype(
        jnp.bfloat16
    )
    input_grad = jnp.transpose(input_grad.reshape(imp_count, table_count, emb_width), (1, 0, 2))
    outgoing = lax.map(
        lambda pair: place_rows(pair[0], pair[1], slot_total).astype(jnp.bfloat16),
        (slot_of, input_grad),
    )
    incoming = lax.all_to_all(
        outgoing.reshape(table_count, owners, capacity, emb_width),
        "table",
        split_axis=1,
        concat_axis=1,
        tiled=True,
    )
    summed = lax.map(
        lambda pair: place_rows(pair[0], pair[1], shard_rows),
        (
            requested.reshape(table_count, slot_total),
            incoming.reshape(table_count, slot_total, emb_width),
        ),
    )
    own_rows = lax.psum_scatter(summed, "dp", scatter_dimension=1, tiled=True)
    emb_step = own_rows / (jnp.sqrt(jnp.mean(own_rows * own_rows, axis=2, keepdims=True)) + 1e-06)
    param_count = w_hidden.size + bias_hidden.size + w_score.size
    weight_tot, bias_tot, score_tot, loss_tot = lax.psum(
        (weight_grad, bias_grad, score_weight_grad, loss_sum), ("table", "dp")
    )
    mean_sq = (
        jnp.sum(weight_tot * weight_tot)
        + jnp.sum(bias_tot * bias_tot)
        + jnp.sum(score_tot * score_tot)
    ) / param_count
    factor = 1.0 / jnp.sqrt(mean_sq + 1e-06)
    step_hidden = weight_tot * factor
    loss = loss_tot / (SESS_DEV * devices)
    return (emb_step, step_hidden, bias_tot * factor, score_tot * factor, loss)


def solution(mesh):
    in_specs = (
        P(None, "table", None),
        P(("table", "dp"), None, None, None),
        P(("table", "dp"), None, None),
        P(("table", "dp"), None),
        P(("table", "dp"), None),
        P(("table", "dp"), None),
        P(),
        P(),
        P(),
    )
    out_specs = (P(None, ("table", "dp"), None), P(), P(), P(), P())
    return jax.shard_map(
        on_device, mesh=mesh, in_specs=in_specs, out_specs=out_specs, check_vma=False
    )
```

profile of v0, /device:TPU:0, one launch (start us, length us, event | category | flops | bytes accessed | tf_op | source)
XLA Modules:
  0.0 230.8 jit_solution(7807377824483772021)
XLA Ops:
  8.0 0.7 copy.45
  8.9 0.7 convert_add_fusion
  9.6 1.2 convert_reduce_fusion
  10.9 0.7 reshape.88
  11.6 8.3 %all-to-all-start = ((s32[16,1,128]{2,1,0:T(1,128)}), s32[16,1,128]{2,1,0:T(1,128)S(1)}, u32[]{:S(2)}, u32[]{:S(2)}) async-start(s32[16,1,128]{2,1,0:T(1,128)} %reshape.88), calls=%async_computation | async-start | bytes 16384 | tf_op jit(solution)/shard_map/all_to_all | solution.py:70
  20.0 7.2 %all-to-all-done = s32[16,1,128]{2,1,0:T(1,128)S(1)} async-done(((s32[16,1,128]{2,1,0:T(1,128)}), s32[16,1,128]{2,1,0:T(1,128)S(1)}, u32[]{:S(2)}, u32[]{:S(2)}) %all-to-all-start) | async-done | bytes 8224 | tf_op jit(solution)/shard_map/all_to_all | solution.py:70
  27.7 0.7 reduce
  28.7 11.4 %while.40 = (s32[]{:T(128)}, bf16[4,512,128]{2,1,0:T(8,128)(2,1)S(1)}, s32[4,512]{1,0:T(4,128)S(1)}, bf16[4,4096,128]{2,1,0:T(8,128)(2,1)}, s32[]{:T(128)}) while((s32[]{:T(128)}, bf16[4,512,128]{2,1,0:T(8,128)(2,1)S(1)}, s32[4,512]{1,0:T(4,128)S(1)}, bf16[4,4096,128]{2,1,0:T(8,128)(2,1)}, s32[]{:T(128)}) %tuple.66), condition=%wide.region_4.5_spmd, body=%wide.region_3.4_spmd.sunk | while | flops 539033600 | bytes 1186889 | solution.py:77
  28.7 2.8 %fusion.58 = bf16[4,512,128]{2,1,0:T(8,128)(2,1)S(1)} fusion(bf16[4,512,128]{2,1,0:T(8,128)(2,1)S(1)} %get-tuple-element.248, s32[]{:T(128)S(6)} %copy.55, s32[512]{0:T(512)S(1)} %bitcast.108, bf16[4,4096,128]{2,1,0:T(8,128)(2,1)} %get-tuple-element.255), kind=kOutput, calls=%fused_computation.5.clone.1 | convolution fusion | flops 539033600 | bytes 1182720 | tf_op jit(solution)/shard_map/while/body/eval_jaxpr/dot_general | solution.py:35
  31.5 2.8 %fusion.58 = bf16[4,512,128]{2,1,0:T(8,128)(2,1)S(1)} fusion(bf16[4,512,128]{2,1,0:T(8,128)(2,1)S(1)} %get-tuple-element.248, s32[]{:T(128)S(6)} %copy.55, s32[512]{0:T(512)S(1)} %bitcast.108, bf16[4,4096,128]{2,1,0:T(8,128)(2,1)} %get-tuple-element.255), kind=kOutput, calls=%fused_computation.5.clone.1 | convolution fusion | flops 539033600 | bytes 1182720 | tf_op jit(solution)/shard_map/while/body/eval_jaxpr/dot_general | solution.py:35
  34.4 2.8 %fusion.58 = bf16[4,512,128]{2,1,0:T(8,128)(2,1)S(1)} fusion(bf16[4,512,128]{2,1,0:T(8,128)(2,1)S(1)} %get-tuple-element.248, s32[]{:T(128)S(6)} %copy.55, s32[512]{0:T(512)S(1)} %bitcast.108, bf16[4,4096,128]{2,1,0:T(8,128)(2,1)} %get-tuple-element.255), kind=kOutput, calls=%fused_computation.5.clone.1 | convolution fusion | flops 539033600 | bytes 1182720 | tf_op jit(solution)/shard_map/while/body/eval_jaxpr/dot_general | solution.py:35
  37.2 2.8 %fusion.58 = bf16[4,512,128]{2,1,0:T(8,128)(2,1)S(1)} fusion(bf16[4,512,128]{2,1,0:T(8,128)(2,1)S(1)} %get-tuple-element.248, s32[]{:T(128)S(6)} %copy.55, s32[512]{0:T(512)S(1)} %bitcast.108, bf16[4,4096,128]{2,1,0:T(8,128)(2,1)} %get-tuple-element.255), kind=kOutput, calls=%fused_computation.5.clone.1 | convolution fusion | flops 539033600 | bytes 1182720 | tf_op jit(solution)/shard_map/while/body/eval_jaxpr/dot_general | solution.py:35
  40.1 0.9 copy.29
  40.9 3.6 %all-to-all-start.1 = ((bf16[4,16,32,128]{3,2,0,1:T(8,128)(2,1)}), bf16[4,16,32,128]{3,2,0,1:T(8,128)(2,1)S(1)}, u32[]{:S(2)}, u32[]{:S(2)}) async-start(bf16[4,16,32,128]{3,2,0,1:T(8,128)(2,1)} %copy.29), calls=%async_computation.1 | async-start | bytes 1048576 | tf_op jit(solution)/shard_map/all_to_all | solution.py:83
  44.5 13.9 %all-to-all-done.1 = bf16[4,16,32,128]{3,2,0,1:T(8,128)(2,1)S(1)} async-done(((bf16[4,16,32,128]{3,2,0,1:T(8,128)(2,1)}), bf16[4,16,32,128]{3,2,0,1:T(8,128)(2,1)S(1)}, u32[]{:S(2)}, u32[]{:S(2)}) %all-to-all-start.1) | async-done | bytes 524320 | tf_op jit(solution)/shard_map/all_to_all | solution.py:83
  58.5 1.8 while.41
  63.0 1.9 while.42
  64.8 0.9 copy.33
  65.7 3.8 %all-to-all-start.2 = ((bf16[4,16,32,128]{3,2,0,1:T(8,128)(2,1)}), bf16[4,16,32,128]{3,2,0,1:T(8,128)(2,1)S(1)}, u32[]{:S(2)}, u32[]{:S(2)}) async-start(bf16[4,16,32,128]{3,2,0,1:T(8,128)(2,1)} %copy.33), calls=%async_computation.2 | async-start | bytes 1048576 | tf_op jit(solution)/shard_map/all_to_all | solution.py:108
  69.5 1.4 fusion.34
  71.1 12.4 %all-to-all-done.2 = bf16[4,16,32,128]{3,2,0,1:T(8,128)(2,1)S(1)} async-done(((bf16[4,16,32,128]{3,2,0,1:T(8,128)(2,1)}), bf16[4,16,32,128]{3,2,0,1:T(8,128)(2,1)S(1)}, u32[]{:S(2)}, u32[]{:S(2)}) %all-to-all-start.2) | async-done | bytes 524320 | tf_op jit(solution)/shard_map/all_to_all | solution.py:108
  83.5 15.1 %while.43 = (s32[]{:T(128)}, f32[4,4096,128]{2,1,0:T(8,128)}, s32[4,512]{1,0:T(4,128)S(1)}, bf16[4,512,128]{2,1,0:T(8,128)(2,1)S(1)}, s32[]{:T(128)}) while((s32[]{:T(128)}, f32[4,4096,128]{2,1,0:T(8,128)}, s32[4,512]{1,0:T(4,128)S(1)}, bf16[4,512,128]{2,1,0:T(8,128)(2,1)S(1)}, s32[]{:T(128)}) %tuple.85), condition=%wide.region_16.17_spmd, body=%wide.region_15.16_spmd.sunk | while | flops 538968064 | bytes 2235465 | solution.py:115
  83.6 3.8 %fusion.64 = f32[4,4096,128]{2,1,0:T(8,128)} fusion(f32[4,4096,128]{2,1,0:T(8,128)} %get-tuple-element.293, s32[]{:T(128)S(6)} %copy.73, s32[512]{0:T(512)S(1)} %bitcast.109, bf16[4,512,128]{2,1,0:T(8,128)(2,1)S(1)} %get-tuple-element.300), kind=kOutput, calls=%fused_computation.31.clone.1 | convolution fusion | flops 538968064 | bytes 2231296 | tf_op jit(solution)/shard_map/while/body/eval_jaxpr/dot_general | solution.py:41
  87.4 3.7 %fusion.64 = f32[4,4096,128]{2,1,0:T(8,128)} fusion(f32[4,4096,128]{2,1,0:T(8,128)} %get-tuple-element.293, s32[]{:T(128)S(6)} %copy.73, s32[512]{0:T(512)S(1)} %bitcast.109, bf16[4,512,128]{2,1,0:T(8,128)(2,1)S(1)} %get-tuple-element.300), kind=kOutput, calls=%fused_computation.31.clone.1 | convolution fusion | flops 538968064 | bytes 2231296 | tf_op jit(solution)/shard_map/while/body/eval_jaxpr/dot_general | solution.py:41
  91.1 3.8 %fusion.64 = f32[4,4096,128]{2,1,0:T(8,128)} fusion(f32[4,4096,128]{2,1,0:T(8,128)} %get-tuple-element.293, s32[]{:T(128)S(6)} %copy.73, s32[512]{0:T(512)S(1)} %bitcast.109, bf16[4,512,128]{2,1,0:T(8,128)(2,1)S(1)} %get-tuple-element.300), kind=kOutput, calls=%fused_computation.31.clone.1 | convolution fusion | flops 538968064 | bytes 2231296 | tf_op jit(solution)/shard_map/while/body/eval_jaxpr/dot_general | solution.py:41
  94.9 3.8 %fusion.64 = f32[4,4096,128]{2,1,0:T(8,128)} fusion(f32[4,4096,128]{2,1,0:T(8,128)} %get-tuple-element.293, s32[]{:T(128)S(6)} %copy.73, s32[512]{0:T(512)S(1)} %bitcast.109, bf16[4,512,128]{2,1,0:T(8,128)(2,1)S(1)} %get-tuple-element.300), kind=kOutput, calls=%fused_computation.31.clone.1 | convolution fusion | flops 538968064 | bytes 2231296 | tf_op jit(solution)/shard_map/while/body/eval_jaxpr/dot_general | solution.py:41
  101.3 39.0 %all-reduce = (f32[512]{0:T(512)S(1)}, f32[512]{0:T(512)S(1)}, f32[]{:T(128)}) all-reduce(f32[512]{0:T(512)S(1)} %fusion.44, f32[512]{0:T(512)S(1)} %bitcast.122, f32[]{:T(128)S(6)} %sub.30), channel_id=1, replica_groups=mesh['table'=16,'dp'=2] {'table','dp'}, use_global_device_ids=true, to_apply=%region_22.23 | all-reduce | flops 1025 | bytes 8200 | tf_op jit(solution)/shard_map/psum | solution.py:125
  141.6 66.5 %all-reduce.3.cloned.1.call-done = f32[512,512]{1,0:T(8,128)} async-done(((f32[512,512]{1,0:T(8,128)}), f32[512,512]{1,0:T(8,128)}) %all-reduce.3.cloned.1.call-update) | async-done | bytes 1048592 | tf_op jit(solution)/shard_map/psum | solution.py:125
  208.1 2.1 multiply_reduce_fusion.1
  213.3 2.3 broadcast_multiply_fusion
  215.6 3.5 %multiply_reduce_fusion = f32[4,2048]{1,0:T(4,128)S(1)} fusion(f32[4,2048,128]{2,1,0:T(8,128)} %reduce-scatter.2.cloned.1.call-done), kind=kLoop, calls=%fused_computation.37 | loop fusion | flops 2088960 | bytes 4227072 | tf_op jit(solution)/shard_map/reduce_sum | solution.py:123
  219.2 3.1 %broadcast_divide_fusion = f32[4,2048,128]{2,1,0:T(8,128)} fusion(f32[4,2048,128]{2,1,0:T(8,128)S(1)} %copy-done, f32[4,2048]{1,0:T(4,128)S(1)} %sqrt_add_fusion), kind=kLoop, calls=%fused_computation.38 | loop fusion | flops 1048576 | bytes 8421376 | tf_op jit(solution)/shard_map/div | solution.py:123
  (84 shorter events, 10.4 us)
Async XLA Ops:
  11.6 15.6 %all-to-all-start = ((s32[16,1,128]{2,1,0:T(1,128)}), s32[16,1,128]{2,1,0:T(1,128)S(1)}, u32[]{:S(2)}, u32[]{:S(2)}) async-start(s32[16,1,128]{2,1,0:T(1,128)} %reshape.88), calls=%async_computation | async-start | bytes 16384 | tf_op jit(solution)/shard_map/all_to_all | solution.py:70
  40.0 20.3 %copy-start.1 = (f32[512,512]{1,0:T(8,128)S(1)}, f32[512,512]{1,0:T(8,128)}, u32[]{:S(2)}) copy-start(f32[512,512]{1,0:T(8,128)} %param.23) | copy-start | bytes 3145732
  40.0 20.3 %copy-start.5 = (f32[512]{0:T(512)S(1)}, f32[512]{0:T(512)}, u32[]{:S(2)}) copy-start(f32[512]{0:T(512)} %param.24) | copy-start | bytes 6148
  40.0 20.6 %copy-start.4 = (f32[512]{0:T(512)S(1)}, f32[512]{0:T(512)}, u32[]{:S(2)}) copy-start(f32[512]{0:T(512)} %param.25) | copy-start | bytes 6148
  40.9 17.6 %all-to-all-start.1 = ((bf16[4,16,32,128]{3,2,0,1:T(8,128)(2,1)}), bf16[4,16,32,128]{3,2,0,1:T(8,128)(2,1)S(1)}, u32[]{:S(2)}, u32[]{:S(2)}) async-start(bf16[4,16,32,128]{3,2,0,1:T(8,128)(2,1)} %copy.29), calls=%async_computation.1 | async-start | bytes 1048576 | tf_op jit(solution)/shard_map/all_to_all | solution.py:83
  44.5 16.8 %copy-start.6 = (f32[1,256]{1,0:T(1,128)S(1)}, f32[1,256]{1,0:T(1,128)}, u32[]{:S(2)}) copy-start(f32[1,256]{1,0:T(1,128)} %param.22) | copy-start | bytes 3076
  44.5 16.8 %copy-start.2 = (s32[1,256]{1,0:T(1,128)S(1)}, s32[1,256]{1,0:T(1,128)}, u32[]{:S(2)}) copy-start(s32[1,256]{1,0:T(1,128)} %param.20) | copy-start | bytes 3076
  44.5 17.0 %copy-start.3 = (f32[1,256]{1,0:T(1,128)S(1)}, f32[1,256]{1,0:T(1,128)}, u32[]{:S(2)}) copy-start(f32[1,256]{1,0:T(1,128)} %param.21) | copy-start | bytes 3076
  65.7 17.8 %all-to-all-start.2 = ((bf16[4,16,32,128]{3,2,0,1:T(8,128)(2,1)}), bf16[4,16,32,128]{3,2,0,1:T(8,128)(2,1)S(1)}, u32[]{:S(2)}, u32[]{:S(2)}) async-start(bf16[4,16,32,128]{3,2,0,1:T(8,128)(2,1)} %copy.33), calls=%async_computation.2 | async-start | bytes 1048576 | tf_op jit(solution)/shard_map/all_to_all | solution.py:108
  69.5 138.6 %all-reduce.3.cloned.1.call-start = ((), (), s32[]{:S(2)}) async-start(), calls=%async_computation.5 | async-start | bytes 2097152 | tf_op jit(solution)/shard_map/psum | solution.py:125
  71.0 144.6 %reduce-scatter.2.cloned.1.call-start = ((), (), s32[]{:S(2)}) async-start(), calls=%async_computation.4 | async-start | bytes 12582912 | tf_op jit(solution)/shard_map/reduce_scatter | solution.py:122
  215.6 3.5 %copy-start = (f32[4,2048,128]{2,1,0:T(8,128)S(1)}, f32[4,2048,128]{2,1,0:T(8,128)}, u32[]{:S(2)}) copy-start(f32[4,2048,128]{2,1,0:T(8,128)} %reduce-scatter.2.cloned.1.call-done) | copy-start | bytes 12582916
Sparse Core Ops, SparseCore 0:
  76.1 131.9 all-reduce.2
Sparse Core Ops, SparseCore 1:
  98.8 14.4 reduce-scatter.1
where the time goes:
time: 232 us; the launch traced here: 231 us
  waiting for transfers between devices  100 us (43%)
  blocking collectives  39 us (17%)
  matrix products  32.6 us (14%)
  between operations  20.8 us (9%)
  other arithmetic  17.3 us (7%)
  starting transfers between devices  15.8 us (7%)
  local copies, waits for them, and re-layouts  4.78 us (2%)
    psum x1, waiting for transfers between devices, on_device(): lax.psum((weight_grad, bias_grad, score_weight_grad, loss_sum), ('table',...  66.5 us
    psum x1, blocking collectives, on_device(): lax.psum((weight_grad, bias_grad, score_weight_grad, loss_sum), ('table',...  39 us
    dot_general x8, matrix products, place_rows(): lax.dot_general(selector(indices, count), values, (((0,), (0,)), ((), ())...  16.8 us
    all_to_all x1, waiting for transfers between devices, on_device(): lax.all_to_all(served, 'table', split_axis=1, concat_axis=1, tiled=True)  13.9 us
    all_to_all x1, waiting for transfers between devices, on_device(): lax.all_to_all(outgoing.reshape(table_count, owners, capacity, emb_width)...  12.4 us
    dot_general x8, matrix products, pick_rows(): jnp.dot(selector(indices, source.shape[0]), source, preferred_element_typ...  12.4 us
    all_to_all x1, starting transfers between devices, on_device(): lax.all_to_all(wanted.reshape(table_count, owners, capacity), 'table', sp...  8.34 us
    all_to_all x1, waiting for transfers between devices, on_device(): lax.all_to_all(wanted.reshape(table_count, owners, capacity), 'table', sp...  7.23 us
  transfers between devices with their start and end apart: 5, of which 4 were waited for; matrix products, arithmetic and copies ran while one was open for 10% of the time, Pallas kernels for 0%

commit v1 on v0

--- a/solution.py
+++ b/solution.py
@@ -105,12 +105,20 @@
         lambda pair: place_rows(pair[0], pair[1], slot_total).astype(jnp.bfloat16),
         (slot_of, input_grad),
     )
-    incoming = lax.all_to_all(
-        outgoing.reshape(table_count, owners, capacity, emb_width),
-        "table",
-        split_axis=1,
-        concat_axis=1,
-        tiled=True,
+    incoming = jnp.concatenate(
+        lax.all_to_all(
+            jnp.stack(
+                jnp.split(
+                    outgoing.reshape(table_count, owners, capacity, emb_width),
+                    lax.axis_size("table"),
+                    axis=1,
+                )
+            ),
+            "table",
+            0,
+            0,
+        ),
+        axis=1,
     )
     summed = lax.map(
         lambda pair: place_rows(pair[0], pair[1], shard_rows),

time: 232 us -> 241 us (1.039)
  local copies, waits for them, and re-layouts: 4.78 us -> 13.8 us
    unnamed x17 -> x32, local copies, waits for them, and re-layouts: 1.51 us -> 10.8 us
where the time goes in v1:
time: 241 us; the launch traced here: 240 us
  waiting for transfers between devices  100 us (41%)
  blocking collectives  39 us (16%)
  matrix products  32.6 us (14%)
  between operations  20.8 us (9%)
  other arithmetic  17.3 us (7%)
  starting transfers between devices  15.8 us (7%)
  local copies, waits for them, and re-layouts  13.8 us (6%)
    psum x1, waiting for transfers between devices, on_device(): lax.psum((weight_grad, bias_grad, score_weight_grad, loss_sum), ('table',...  66.5 us
    psum x1, blocking collectives, on_device(): lax.psum((weight_grad, bias_grad, score_weight_grad, loss_sum), ('table',...  39 us
    dot_general x8, matrix products, place_rows(): lax.dot_general(selector(indices, count), values, (((0,), (0,)), ((), ())...  16.8 us
    all_to_all x1, waiting for transfers between devices, on_device(): lax.all_to_all(served, 'table', split_axis=1, concat_axis=1, tiled=True)  13.9 us
    all_to_all x1, waiting for transfers between devices, on_device(): lax.all_to_all(jnp.stack(jnp.split(outgoing.reshape(table_count, owners,...  12.4 us
    dot_general x8, matrix products, pick_rows(): jnp.dot(selector(indices, source.shape[0]), source, preferred_element_typ...  12.4 us
    unnamed x32, local copies, waits for them, and re-layouts  10.8 us
    all_to_all x1, starting transfers between devices, on_device(): lax.all_to_all(wanted.reshape(table_count, owners, capacity), 'table', sp...  8.34 us
  transfers between devices with their start and end apart: 5, of which 4 were waited for; matrix products, arithmetic and copies ran while one was open for 10% of the time, Pallas kernels for 0%

profile of v1, /device:TPU:0, one launch (start us, length us, event | category | flops | bytes accessed | tf_op | source)
XLA Modules:
  0.0 239.9 jit_solution(7184889849275414496)
XLA Ops:
  8.0 0.7 copy.120
  8.9 0.7 convert_add_fusion
  9.6 1.2 convert_reduce_fusion
  10.9 0.7 reshape.88
  11.6 8.3 %all-to-all-start = ((s32[16,1,128]{2,1,0:T(1,128)}), s32[16,1,128]{2,1,0:T(1,128)S(1)}, u32[]{:S(2)}, u32[]{:S(2)}) async-start(s32[16,1,128]{2,1,0:T(1,128)} %reshape.88), calls=%async_computation | async-start | bytes 16384 | tf_op jit(solution)/shard_map/all_to_all | solution.py:70
  20.0 7.2 %all-to-all-done = s32[16,1,128]{2,1,0:T(1,128)S(1)} async-done(((s32[16,1,128]{2,1,0:T(1,128)}), s32[16,1,128]{2,1,0:T(1,128)S(1)}, u32[]{:S(2)}, u32[]{:S(2)}) %all-to-all-start) | async-done | bytes 8224 | tf_op jit(solution)/shard_map/all_to_all | solution.py:70
  27.7 0.7 reduce
  28.6 11.4 %while.40 = (s32[]{:T(128)}, bf16[4,512,128]{2,1,0:T(8,128)(2,1)S(1)}, s32[4,512]{1,0:T(4,128)S(1)}, bf16[4,4096,128]{2,1,0:T(8,128)(2,1)}, s32[]{:T(128)}) while((s32[]{:T(128)}, bf16[4,512,128]{2,1,0:T(8,128)(2,1)S(1)}, s32[4,512]{1,0:T(4,128)S(1)}, bf16[4,4096,128]{2,1,0:T(8,128)(2,1)}, s32[]{:T(128)}) %tuple.66), condition=%wide.region_4.5_spmd, body=%wide.region_3.4_spmd.sunk | while | flops 539033600 | bytes 1186889 | solution.py:77
  28.7 2.8 %fusion.58 = bf16[4,512,128]{2,1,0:T(8,128)(2,1)S(1)} fusion(bf16[4,512,128]{2,1,0:T(8,128)(2,1)S(1)} %get-tuple-element.248, s32[]{:T(128)S(6)} %copy.130, s32[512]{0:T(512)S(1)} %bitcast.219, bf16[4,4096,128]{2,1,0:T(8,128)(2,1)} %get-tuple-element.255), kind=kOutput, calls=%fused_computation.5.clone.1 | convolution fusion | flops 539033600 | bytes 1182720 | tf_op jit(solution)/shard_map/while/body/eval_jaxpr/dot_general | solution.py:35
  31.5 2.8 %fusion.58 = bf16[4,512,128]{2,1,0:T(8,128)(2,1)S(1)} fusion(bf16[4,512,128]{2,1,0:T(8,128)(2,1)S(1)} %get-tuple-element.248, s32[]{:T(128)S(6)} %copy.130, s32[512]{0:T(512)S(1)} %bitcast.219, bf16[4,4096,128]{2,1,0:T(8,128)(2,1)} %get-tuple-element.255), kind=kOutput, calls=%fused_computation.5.clone.1 | convolution fusion | flops 539033600 | bytes 1182720 | tf_op jit(solution)/shard_map/while/body/eval_jaxpr/dot_general | solution.py:35
  34.4 2.8 %fusion.58 = bf16[4,512,128]{2,1,0:T(8,128)(2,1)S(1)} fusion(bf16[4,512,128]{2,1,0:T(8,128)(2,1)S(1)} %get-tuple-element.248, s32[]{:T(128)S(6)} %copy.130, s32[512]{0:T(512)S(1)} %bitcast.219, bf16[4,4096,128]{2,1,0:T(8,128)(2,1)} %get-tuple-element.255), kind=kOutput, calls=%fused_computation.5.clone.1 | convolution fusion | flops 539033600 | bytes 1182720 | tf_op jit(solution)/shard_map/while/body/eval_jaxpr/dot_general | solution.py:35
  37.2 2.8 %fusion.58 = bf16[4,512,128]{2,1,0:T(8,128)(2,1)S(1)} fusion(bf16[4,512,128]{2,1,0:T(8,128)(2,1)S(1)} %get-tuple-element.248, s32[]{:T(128)S(6)} %copy.130, s32[512]{0:T(512)S(1)} %bitcast.219, bf16[4,4096,128]{2,1,0:T(8,128)(2,1)} %get-tuple-element.255), kind=kOutput, calls=%fused_computation.5.clone.1 | convolution fusion | flops 539033600 | bytes 1182720 | tf_op jit(solution)/shard_map/while/body/eval_jaxpr/dot_general | solution.py:35
  40.1 0.9 copy.75
  40.9 3.6 %all-to-all-start.1 = ((bf16[4,16,32,128]{3,2,0,1:T(8,128)(2,1)}), bf16[4,16,32,128]{3,2,0,1:T(8,128)(2,1)S(1)}, u32[]{:S(2)}, u32[]{:S(2)}) async-start(bf16[4,16,32,128]{3,2,0,1:T(8,128)(2,1)} %copy.75), calls=%async_computation.1 | async-start | bytes 1048576 | tf_op jit(solution)/shard_map/all_to_all | solution.py:83
  44.5 13.9 %all-to-all-done.1 = bf16[4,16,32,128]{3,2,0,1:T(8,128)(2,1)S(1)} async-done(((bf16[4,16,32,128]{3,2,0,1:T(8,128)(2,1)}), bf16[4,16,32,128]{3,2,0,1:T(8,128)(2,1)S(1)}, u32[]{:S(2)}, u32[]{:S(2)}) %all-to-all-start.1) | async-done | bytes 524320 | tf_op jit(solution)/shard_map/all_to_all | solution.py:83
  58.5 1.8 while.41
  62.9 1.9 while.42
  64.8 0.6 constant_dynamic-update-slice_fusion.16
  74.7 3.8 %all-to-all-start.2 = ((bf16[16,4,1,32,128]{4,3,1,2,0:T(8,128)(2,1)}), bf16[16,4,1,32,128]{4,3,1,2,0:T(8,128)(2,1)S(1)}, u32[]{:S(2)}, u32[]{:S(2)}) async-start(bf16[16,4,1,32,128]{4,3,1,2,0:T(8,128)(2,1)} %constant_dynamic-update-slice_fusion.1), calls=%async_computation.2 | async-start | bytes 1048576 | tf_op jit(solution)/shard_map/all_to_all | solution.py:109
  78.6 1.4 fusion.34
  80.1 12.4 %all-to-all-done.2 = bf16[16,4,1,32,128]{4,3,1,2,0:T(8,128)(2,1)S(1)} async-done(((bf16[16,4,1,32,128]{4,3,1,2,0:T(8,128)(2,1)}), bf16[16,4,1,32,128]{4,3,1,2,0:T(8,128)(2,1)S(1)}, u32[]{:S(2)}, u32[]{:S(2)}) %all-to-all-start.2) | async-done | bytes 524320 | tf_op jit(solution)/shard_map/all_to_all | solution.py:109
  92.6 15.1 %while.43 = (s32[]{:T(128)}, f32[4,4096,128]{2,1,0:T(8,128)}, s32[4,512]{1,0:T(4,128)S(1)}, bf16[4,512,128]{2,1,0:T(8,128)(2,1)S(1)}, s32[]{:T(128)}) while((s32[]{:T(128)}, f32[4,4096,128]{2,1,0:T(8,128)}, s32[4,512]{1,0:T(4,128)S(1)}, bf16[4,512,128]{2,1,0:T(8,128)(2,1)S(1)}, s32[]{:T(128)}) %tuple.85), condition=%wide.region_16.17_spmd, body=%wide.region_15.16_spmd.sunk | while | flops 538968064 | bytes 2235465 | solution.py:123
  92.6 3.8 %fusion.64 = f32[4,4096,128]{2,1,0:T(8,128)} fusion(f32[4,4096,128]{2,1,0:T(8,128)} %get-tuple-element.293, s32[]{:T(128)S(6)} %copy.163, s32[512]{0:T(512)S(1)} %bitcast.220, bf16[4,512,128]{2,1,0:T(8,128)(2,1)S(1)} %get-tuple-element.300), kind=kOutput, calls=%fused_computation.31.clone.1 | convolution fusion | flops 538968064 | bytes 2231296 | tf_op jit(solution)/shard_map/while/body/eval_jaxpr/dot_general | solution.py:41
  96.4 3.7 %fusion.64 = f32[4,4096,128]{2,1,0:T(8,128)} fusion(f32[4,4096,128]{2,1,0:T(8,128)} %get-tuple-element.293, s32[]{:T(128)S(6)} %copy.163, s32[512]{0:T(512)S(1)} %bitcast.220, bf16[4,512,128]{2,1,0:T(8,128)(2,1)S(1)} %get-tuple-element.300), kind=kOutput, calls=%fused_computation.31.clone.1 | convolution fusion | flops 538968064 | bytes 2231296 | tf_op jit(solution)/shard_map/while/body/eval_jaxpr/dot_general | solution.py:41
  100.1 3.8 %fusion.64 = f32[4,4096,128]{2,1,0:T(8,128)} fusion(f32[4,4096,128]{2,1,0:T(8,128)} %get-tuple-element.293, s32[]{:T(128)S(6)} %copy.163, s32[512]{0:T(512)S(1)} %bitcast.220, bf16[4,512,128]{2,1,0:T(8,128)(2,1)S(1)} %get-tuple-element.300), kind=kOutput, calls=%fused_computation.31.clone.1 | convolution fusion | flops 538968064 | bytes 2231296 | tf_op jit(solution)/shard_map/while/body/eval_jaxpr/dot_general | solution.py:41
  103.9 3.8 %fusion.64 = f32[4,4096,128]{2,1,0:T(8,128)} fusion(f32[4,4096,128]{2,1,0:T(8,128)} %get-tuple-element.293, s32[]{:T(128)S(6)} %copy.163, s32[512]{0:T(512)S(1)} %bitcast.220, bf16[4,512,128]{2,1,0:T(8,128)(2,1)S(1)} %get-tuple-element.300), kind=kOutput, calls=%fused_computation.31.clone.1 | convolution fusion | flops 538968064 | bytes 2231296 | tf_op jit(solution)/shard_map/while/body/eval_jaxpr/dot_general | solution.py:41
  110.3 39.0 %all-reduce = (f32[512]{0:T(512)S(1)}, f32[512]{0:T(512)S(1)}, f32[]{:T(128)}) all-reduce(f32[512]{0:T(512)S(1)} %fusion.44, f32[512]{0:T(512)S(1)} %bitcast.233, f32[]{:T(128)S(6)} %sub.30), channel_id=1, replica_groups=mesh['table'=16,'dp'=2] {'table','dp'}, use_global_device_ids=true, to_apply=%region_22.23 | all-reduce | flops 1025 | bytes 8200 | tf_op jit(solution)/shard_map/psum | solution.py:133
  150.6 66.5 %all-reduce.3.cloned.1.call-done = f32[512,512]{1,0:T(8,128)} async-done(((f32[512,512]{1,0:T(8,128)}), f32[512,512]{1,0:T(8,128)}) %all-reduce.3.cloned.1.call-update) | async-done | bytes 1048592 | tf_op jit(solution)/shard_map/psum | solution.py:133
  217.1 2.1 multiply_reduce_fusion.1
  222.4 2.3 broadcast_multiply_fusion
  224.6 3.5 %multiply_reduce_fusion = f32[4,2048]{1,0:T(4,128)S(1)} fusion(f32[4,2048,128]{2,1,0:T(8,128)} %reduce-scatter.2.cloned.1.call-done), kind=kLoop, calls=%fused_computation.37 | loop fusion | flops 2088960 | bytes 4227072 | tf_op jit(solution)/shard_map/reduce_sum | solution.py:131
  228.2 3.1 %broadcast_divide_fusion = f32[4,2048,128]{2,1,0:T(8,128)} fusion(f32[4,2048,128]{2,1,0:T(8,128)S(1)} %copy-done, f32[4,2048]{1,0:T(4,128)S(1)} %sqrt_add_fusion), kind=kLoop, calls=%fused_computation.38 | loop fusion | flops 1048576 | bytes 8421376 | tf_op jit(solution)/shard_map/div | solution.py:131
  (99 shorter events, 19.6 us)
Async XLA Ops:
  11.6 15.6 %all-to-all-start = ((s32[16,1,128]{2,1,0:T(1,128)}), s32[16,1,128]{2,1,0:T(1,128)S(1)}, u32[]{:S(2)}, u32[]{:S(2)}) async-start(s32[16,1,128]{2,1,0:T(1,128)} %reshape.88), calls=%async_computation | async-start | bytes 16384 | tf_op jit(solution)/shard_map/all_to_all | solution.py:70
  40.0 20.3 %copy-start.1 = (f32[512,512]{1,0:T(8,128)S(1)}, f32[512,512]{1,0:T(8,128)}, u32[]{:S(2)}) copy-start(f32[512,512]{1,0:T(8,128)} %param.23) | copy-start | bytes 3145732
  40.0 20.3 %copy-start.5 = (f32[512]{0:T(512)S(1)}, f32[512]{0:T(512)}, u32[]{:S(2)}) copy-start(f32[512]{0:T(512)} %param.24) | copy-start | bytes 6148
  40.0 20.6 %copy-start.4 = (f32[512]{0:T(512)S(1)}, f32[512]{0:T(512)}, u32[]{:S(2)}) copy-start(f32[512]{0:T(512)} %param.25) | copy-start | bytes 6148
  40.9 17.6 %all-to-all-start.1 = ((bf16[4,16,32,128]{3,2,0,1:T(8,128)(2,1)}), bf16[4,16,32,128]{3,2,0,1:T(8,128)(2,1)S(1)}, u32[]{:S(2)}, u32[]{:S(2)}) async-start(bf16[4,16,32,128]{3,2,0,1:T(8,128)(2,1)} %copy.75), calls=%async_computation.1 | async-start | bytes 1048576 | tf_op jit(solution)/shard_map/all_to_all | solution.py:83
  44.5 16.8 %copy-start.6 = (f32[1,256]{1,0:T(1,128)S(1)}, f32[1,256]{1,0:T(1,128)}, u32[]{:S(2)}) copy-start(f32[1,256]{1,0:T(1,128)} %param.22) | copy-start | bytes 3076
  44.5 16.8 %copy-start.2 = (s32[1,256]{1,0:T(1,128)S(1)}, s32[1,256]{1,0:T(1,128)}, u32[]{:S(2)}) copy-start(s32[1,256]{1,0:T(1,128)} %param.20) | copy-start | bytes 3076
  44.5 17.0 %copy-start.3 = (f32[1,256]{1,0:T(1,128)S(1)}, f32[1,256]{1,0:T(1,128)}, u32[]{:S(2)}) copy-start(f32[1,256]{1,0:T(1,128)} %param.21) | copy-start | bytes 3076
  74.7 17.8 %all-to-all-start.2 = ((bf16[16,4,1,32,128]{4,3,1,2,0:T(8,128)(2,1)}), bf16[16,4,1,32,128]{4,3,1,2,0:T(8,128)(2,1)S(1)}, u32[]{:S(2)}, u32[]{:S(2)}) async-start(bf16[16,4,1,32,128]{4,3,1,2,0:T(8,128)(2,1)} %constant_dynamic-update-slice_fusion.1), calls=%async_computation.2 | async-start | bytes 1048576 | tf_op jit(solution)/shard_map/all_to_all | solution.py:109
  78.5 138.6 %all-reduce.3.cloned.1.call-start = ((), (), s32[]{:S(2)}) async-start(), calls=%async_computation.5 | async-start | bytes 2097152 | tf_op jit(solution)/shard_map/psum | solution.py:133
  80.0 144.6 %reduce-scatter.2.cloned.1.call-start = ((), (), s32[]{:S(2)}) async-start(), calls=%async_computation.4 | async-start | bytes 12582912 | tf_op jit(solution)/shard_map/reduce_scatter | solution.py:130
  224.6 3.5 %copy-start = (f32[4,2048,128]{2,1,0:T(8,128)S(1)}, f32[4,2048,128]{2,1,0:T(8,128)}, u32[]{:S(2)}) copy-start(f32[4,2048,128]{2,1,0:T(8,128)} %reduce-scatter.2.cloned.1.call-done) | copy-start | bytes 12582916
Sparse Core Ops, SparseCore 0:
  85.1 131.9 all-reduce.2
Sparse Core Ops, SparseCore 1:
  107.8 14.4 reduce-scatter.1
